TPU v7x, 32 devices: a whole 2x2x4 slice. The times are simulated.
32 devices in a mesh: sp: 2 (over core), py: 4 (over z), pz: 4 (over y, x).
Axes of the slice: x: 2, y: 2, z: 4, core: 2. Of those that a mesh axis runs over, the one named last changes fastest.
Arguments:
- concentration: float32 [8, 128, 128, 128], P('sp', 'py', 'pz'), may hold values from -1 to 1.1
- mobility: float32 [8, 8], replicated, may hold values from 0.1 to 0.6
- kappa: float32 [8], replicated, may hold values from 0.5 to 2
- well_depth: float32 [8], P('sp'), may hold values from 0.5 to 2
Outputs:
- updated: float32 [8, 128, 128, 128], P('sp', 'py', 'pz')
All inputs are finite; a program needn't handle non-finite values.
Results may differ from a plain program's by a relative error of at most 0.000084.
Values sent between devices are 32-bit elements; how exact they have to be, the bound alone decides.
A program may use at most 128 MiB of HBM per device.

v0:
```python
import math

import jax
import jax.numpy as jnp
from jax import lax
from jax.sharding import PartitionSpec as P


def tables(count):
    modes = jnp.arange(count, dtype=jnp.int32)
    product = modes[:, None] * modes[None, :] % count
    angle = 2.0 * math.pi * product.astype(jnp.float32) / count
    return (jnp.cos(angle), jnp.sin(angle))


def wave_square(index, count):
    freq = jnp.where(index < count // 2, index, index - count).astype(jnp.float32)
    return (2.0 * math.pi * freq / count) ** 2


def contract(form, values, table):
    return jnp.einsum(form, values, table, precision=lax.Precision.HIGHEST)


def rotate(spectrum, form, count, forward):
    cosine, sine = tables(count)
    real_part, imag_part = (spectrum[0], spectrum[1])
    real_cos = contract(form, real_part, cosine)
    real_sin = contract(form, real_part, sine)
    imag_cos = contract(form, imag_part, cosine)
    imag_sin = contract(form, imag_part, sine)
    if forward:
        return jnp.stack([real_cos + imag_sin, imag_cos - real_sin])
    return jnp.stack([real_cos - imag_sin, imag_cos + real_sin])


def per_device(concentration, mobility, kappa, well_depth):
    local_species, rows_x, rows_y, depth = concentration.shape
    count_sp = lax.axis_size("sp")
    count_py = lax.axis_size("py")
    count_pz = lax.axis_size("pz")
    full_x = rows_x * count_py
    full_y = rows_y * count_pz
    half_depth = depth // 2
    bulk = well_depth[:, None, None, None] * (
        concentration * concentration * concentration - concentration
    )
    fields = jnp.stack([concentration, bulk])
    cosine, sine = tables(depth)
    alternate = (1 - 2 * (jnp.arange(depth, dtype=jnp.int32) % 2)).astype(jnp.float32)
    spectrum = jnp.stack(
        [
            contract("fsxyz,zk->fsxyk", fields, cosine[:, :half_depth]),
            -contract("fsxyz,zk->fsxyk", fields, sine[:, :half_depth]),
        ]
    )
    spectrum = lax.all_to_all(spectrum, "pz", split_axis=5, concat_axis=4, tiled=True)
    own_lines = spectrum.shape[5]
    highest = contract("fsxyz,z->fsxy", fields, alternate)
    highest = lax.all_gather(highest, "pz", axis=3, tiled=True)
    highest = jnp.stack([highest, jnp.zeros_like(highest)])[..., None]
    spectrum = jnp.concatenate([spectrum, highest], axis=5)
    z_modes = jnp.concatenate(
        [
            lax.axis_index("pz") * own_lines + jnp.arange(own_lines, dtype=jnp.int32),
            jnp.full((1,), half_depth, jnp.int32),
        ]
    )
    spectrum = rotate(spectrum, "fsxyz,yk->fsxkz", full_y, True)
    spectrum = lax.all_to_all(
        lax.all_to_all(spectrum, "sp", split_axis=4, concat_axis=2, tiled=True),
        "py",
        split_axis=4,
        concat_axis=3,
        tiled=True,
    )
    spectrum = rotate(spectrum, "fsxyz,xk->fskyz", full_x, True)
    narrow = spectrum.shape[4]
    lines = spectrum.shape[5]
    y_start = (lax.axis_index("sp") * count_py + lax.axis_index("py")) * narrow
    ksq_x = wave_square(jnp.arange(full_x, dtype=jnp.int32), full_x)
    ksq_y = wave_square(y_start + jnp.arange(narrow, dtype=jnp.int32), full_y)
    ksq_z = wave_square(z_modes, depth)
    ksq = ksq_x[:, None, None] + ksq_y[None, :, None] + ksq_z[None, None, :]
    c_hat = spectrum[:, 0]
    drive = spectrum[:, 1] + kappa[None, :, None, None, None] * ksq[None, None] * c_hat
    mix = jnp.einsum("ij,rjxyz->rixyz", mobility, drive, precision=lax.Precision.HIGHEST)
    stiff = 0.5 * (jnp.diagonal(mobility) * kappa)[:, None, None, None] * (ksq * ksq)[None]
    new_hat = (c_hat * (1.0 + stiff)[None] - 0.5 * ksq[None, None] * mix) / (1.0 + stiff)[None]
    new_hat = rotate(new_hat, "sxyz,xk->skyz", full_x, False)
    moved = lax.all_to_all(
        lax.all_to_all(new_hat, "sp", split_axis=1, concat_axis=3, tiled=True),
        "py",
        split_axis=2,
        concat_axis=3,
        tiled=True,
    )
    moved = moved.reshape(2, local_species, rows_x, count_py, count_sp, narrow, lines)
    moved = moved.transpose(0, 1, 2, 4, 3, 5, 6).reshape(2, local_species, rows_x, full_y, lines)
    moved = rotate(moved, "sxyz,yk->sxkz", full_y, False)
    main = moved[..., : lines - 1]
    highest = moved[0, :, :, :, lines - 1]
    main = lax.all_to_all(main, "pz", split_axis=3, concat_axis=4, tiled=True)
    highest = lax.dynamic_slice_in_dim(highest, lax.axis_index("pz") * rows_y, rows_y, 2)
    weight = jnp.where(jnp.arange(half_depth, dtype=jnp.int32) == 0, 1.0, 2.0).astype(jnp.float32)
    result = contract("sxyk,kz->sxyz", main[0] * weight, cosine[:half_depth]) - contract(
        "sxyk,kz->sxyz", main[1] * weight, sine[:half_depth]
    )
    result = result + highest[..., None] * alternate[None, None, None, :]
    return result * (1.0 / (full_x * full_y * depth))


def solution(mesh):
    in_specs = (P("sp", "py", "pz", None), P(), P(), P("sp"))
    out_specs = P("sp", "py", "pz", None)
    return jax.shard_map(
        per_device, mesh=mesh, in_specs=in_specs, out_specs=out_specs, check_vma=False
    )
```

profile of v0, /device:TPU:0, one launch (start us, length us, event | category | flops | bytes accessed | tf_op | source)
XLA Modules:
  0.0 783.9 jit_solution(356317510580128092)
XLA Ops:
  13.9 16.6 %copy.169 = f32[2,2,4,32,32,64]{4,3,2,1,0,5:T(8,128)} copy(f32[2,2,4,32,32,64]{5,4,3,2,1,0:T(8,128)} %pad_maximum_fusion) | data formatting | bytes 8388608 | tf_op jit(solution)/shard_map/stack | solution.py:51
  30.5 11.5 %reshape.175 = f32[4,1,262144]{2,1,0:T(1,128)} reshape(f32[64,2,2,4,32,32]{5,4,3,2,1,0:T(8,128)} %bitcast.208) | data formatting | bytes 8388608
  47.2 17.9 %fusion.9 = f32[1,2,4,32,32]{4,0,3,2,1:T(1,128)S(1)} fusion(f32[1,4,32,32,128]{4,3,2,1,0:T(8,128)} %copy-done.3, f32[1,4,32,32,128]{4,3,2,1,0:T(8,128)S(1)} %bitcast.224), kind=kOutput, calls=%fused_computation.25 | convolution fusion | flops 13632640 | bytes 4227072 | tf_op jit(solution)/shard_map/fsxyz,z->fsxy/dot_general | solution.py:22
  65.2 36.4 %all_gather.3 = f32[2,4,32,128]{2,1,0,3:T(4,128)S(1)} all-gather(f32[2,4,32,32]{2,1,0,3:T(4,128)S(1)} %bitcast.230), channel_id=1, replica_groups=mesh['sp'=2,'py'=4,'pz'=4] {'pz'}, dimensions={3}, use_global_device_ids=true | all-gather | bytes 163840 | tf_op jit(solution)/shard_map/all_gather | solution.py:60
  102.4 16.1 %reduce = f32[4,262144]{1,0:T(4,128)} reduce(f32[4,1,262144]{2,1,0:T(1,128)} %all-to-all-done, f32[]{:T(128)} %broadcast.307), dimensions={1}, to_apply=%all_to_all.72.reduce_sub_computation | reduce | bytes 8388612 | tf_op jit(solution)/shard_map/all_to_all | solution.py:57
  118.5 13.7 %reshape.176 = f32[64,2,2,4,32,32]{5,4,3,2,1,0:T(8,128)} reshape(f32[4,262144]{1,0:T(4,128)} %reduce) | data formatting | bytes 8388608
  132.2 21.0 %copy.171 = f32[2,2,4,32,4,32,16]{5,4,3,6,2,1,0:T(4,128)} copy(f32[2,2,4,32,4,32,16]{5,3,2,1,0,6,4:T(8,128)} %bitcast.209) | data formatting | bytes 8388608 | tf_op jit(solution)/shard_map/all_to_all | solution.py:57
  153.2 13.6 %all_to_all.75 = f32[2,2,4,32,128,16]{4,3,5,2,1,0:T(8,128)} reshape(f32[2,2,4,32,4,32,16]{5,4,3,6,2,1,0:T(4,128)} %copy.171) | data formatting | bytes 8388608 | tf_op jit(solution)/shard_map/all_to_all | solution.py:57
  180.4 15.2 %copy.177 = f32[2,2,4,32,128,17]{3,2,5,1,0,4:T(4,128)} copy(f32[2,2,4,32,128,17]{4,3,5,2,1,0:T(8,128)} %pad_maximum_fusion.1) | data formatting | bytes 8912896 | tf_op jit(solution)/shard_map/stack | solution.py:33
  195.6 22.2 %reshape.177 = f32[2,1,557056]{2,1,0:T(1,128)} reshape(f32[128,2,2,17,4,32]{5,4,3,2,1,0:T(4,128)} %bitcast.204) | data formatting | bytes 8912896
  217.8 12.4 %all_to_all.99 = f32[2,1,557056]{2,1,0:T(1,128)} all-to-all(f32[2,1,557056]{2,1,0:T(1,128)} %reshape.177), channel_id=1, replica_groups=mesh['sp'=2,'py'=4,'pz'=4] {'sp'}, dimensions={0} | all-to-all | bytes 8912896 | tf_op jit(solution)/shard_map/all_to_all | solution.py:71
  230.2 17.5 %reduce.1 = f32[2,557056]{1,0:T(2,128)} reduce(f32[2,1,557056]{2,1,0:T(1,128)} %all_to_all.99, f32[]{:T(128)} %broadcast.307), dimensions={1}, to_apply=%all_to_all.76.reduce_sub_computation | reduce | bytes 8912900 | tf_op jit(solution)/shard_map/all_to_all | solution.py:71
  247.7 23.0 %reshape.178 = f32[128,2,2,17,4,32]{5,4,3,2,1,0:T(4,128)} reshape(f32[2,557056]{1,0:T(2,128)} %reduce.1) | data formatting | bytes 8912896
  270.7 20.5 %copy.258 = f32[2,2,4,32,2,64,17]{5,4,3,6,2,1,0:T(2,128)} copy(f32[2,2,4,32,2,64,17]{3,2,6,1,0,5,4:T(4,128)} %bitcast.205) | data formatting | bytes 8912896 | tf_op jit(solution)/shard_map/all_to_all | solution.py:71
  291.2 8.3 %copy.179 = f32[2,2,2,4,32,64,17]{5,4,6,3,2,1,0:T(8,128)} copy(f32[2,2,2,4,32,64,17]{5,2,4,6,3,1,0:T(2,128)} %bitcast.215) | data formatting | bytes 8912896 | tf_op jit(solution)/shard_map/all_to_all | solution.py:71
  299.5 17.6 %copy.180 = f32[2,2,8,32,64,17]{3,2,5,1,0,4:T(8,128)} copy(f32[2,2,8,32,64,17]{4,3,5,2,1,0:T(8,128)} %bitcast.216) | data formatting | bytes 8912896 | tf_op jit(solution)/shard_map/all_to_all | solution.py:71
  317.0 21.0 %reshape.179 = f32[4,1,278528]{2,1,0:T(1,128)} reshape(f32[64,2,2,17,8,32]{5,4,3,2,1,0:T(8,128)} %bitcast.206) | data formatting | bytes 8912896
  346.1 96.4 %all-to-all-done.2 = f32[4,1,278528]{2,1,0:T(1,128)} async-done(((f32[4,1,278528]{2,1,0:T(1,128)}), f32[4,1,278528]{2,1,0:T(1,128)}, u32[]{:S(2)}, u32[]{:S(2)}) %all-to-all-start.2) | async-done | bytes 4456480 | tf_op jit(solution)/shard_map/all_to_all | solution.py:70
  442.5 16.0 %reduce.2 = f32[4,278528]{1,0:T(4,128)} reduce(f32[4,1,278528]{2,1,0:T(1,128)} %all-to-all-done.2, f32[]{:T(128)} %broadcast.307), dimensions={1}, to_apply=%all_to_all.80.reduce_sub_computation | reduce | bytes 8912900 | tf_op jit(solution)/shard_map/all_to_all | solution.py:70
  458.5 14.6 %reshape.180 = f32[64,2,2,17,8,32]{5,4,3,2,1,0:T(8,128)} reshape(f32[4,278528]{1,0:T(4,128)} %reduce.2) | data formatting | bytes 8912896
  473.1 9.9 %copy.181 = f32[2,2,8,32,64,17]{3,4,5,2,1,0:T(8,128)S(1)} copy(f32[2,2,8,32,64,17]{3,2,5,1,0,4:T(8,128)} %bitcast.207) | data formatting | bytes 8912896 | tf_op jit(solution)/shard_map/all_to_all | solution.py:70
  490.5 10.5 %copy.273 = f32[1,2,8,4,32,16,17]{4,3,6,5,2,1,0:T(4,128)} copy(f32[1,2,8,4,32,16,17]{4,5,3,6,2,1,0:T(8,128)} %get-tuple-element.5) | data formatting | bytes 4456448 | tf_op jit(solution)/shard_map/squeeze | solution.py:27
  513.0 10.4 %copy.274 = f32[1,2,8,4,32,16,17]{4,3,6,5,2,1,0:T(4,128)} copy(f32[1,2,8,4,32,16,17]{4,5,3,6,2,1,0:T(8,128)} %get-tuple-element.6) | data formatting | bytes 4456448 | tf_op jit(solution)/shard_map/squeeze | solution.py:27
  523.4 8.9 %reshape.174 = f32[2,8,128,16,17]{2,4,3,1,0:T(8,128)} reshape(f32[1,2,8,4,32,16,17]{4,3,6,5,2,1,0:T(4,128)} %copy.274) | data formatting | bytes 4456448 | tf_op jit(solution)/shard_map/squeeze | solution.py:27
  568.4 7.7 reshape.181
  576.2 55.0 %all_to_all.101 = f32[4,1,139264]{2,1,0:T(1,128)} all-to-all(f32[4,1,139264]{2,1,0:T(1,128)S(1)} %reshape.181), channel_id=1, replica_groups=mesh['sp'=2,'py'=4,'pz'=4] {'py'}, dimensions={0} | all-to-all | bytes 4456448 | tf_op jit(solution)/shard_map/all_to_all | solution.py:91
  639.0 8.3 %reshape.182 = f32[128,2,17,4,32]{4,3,2,1,0:T(4,128)} reshape(f32[4,139264]{1,0:T(4,128)S(1)} %reduce.3) | data formatting | bytes 4456448
  647.3 12.1 %copy.204 = f32[2,4,32,4,32,17]{2,4,5,3,1,0:T(8,128)} copy(f32[2,4,32,4,32,17]{4,1,5,0,2,3:T(4,128)} %bitcast.218) | data formatting | bytes 4456448 | tf_op jit(solution)/shard_map/all_to_all | solution.py:91
  694.3 7.9 %copy.215 = f32[2,4,32,128,16]{2,4,1,0,3:T(8,128)} copy(f32[2,4,32,128,16]{3,2,4,1,0:T(8,128)S(1)} %pad_maximum_fusion.13) | data formatting | bytes 4194304 | tf_op jit(solution)/shard_map/slice | solution.py:101
  713.9 24.5 %all-to-all-done.5 = f32[4,1,131072]{2,1,0:T(1,128)} async-done(((f32[4,1,131072]{2,1,0:T(1,128)}), f32[4,1,131072]{2,1,0:T(1,128)}, u32[]{:S(2)}, u32[]{:S(2)}) %all-to-all-start.5) | async-done | bytes 2097184 | tf_op jit(solution)/shard_map/all_to_all | solution.py:103
  752.2 11.8 %copy.216 = f32[2,4,32,4,32,16]{4,5,3,2,1,0:T(8,128)} copy(f32[2,4,32,4,32,16]{2,5,1,0,4,3:T(8,128)} %bitcast.220) | data formatting | bytes 4194304 | tf_op jit(solution)/shard_map/all_to_all | solution.py:103
  775.2 8.6 %add_multiply_fusion = f32[4,32,32,128]{3,2,1,0:T(8,128)} fusion(f32[4,32,32,128]{3,2,1,0:T(8,128)S(1)} %fusion, f32[4,32,32,64]{2,3,1,0:T(8,128)S(1)} %bitcast.225, f32[64]{0:T(128)S(1)} %compare_select_fusion.3, f32[128]{0:T(128)S(1)} %fusion.81, f32[4,32,32]{2,1,0:T(8,128)S(1)} %dynamic-slice_bitcast_fusion, f32[128,128]{0,1:T(8,128)S(1)} %copy-done.9), kind=kOutput, calls=%fused_computation.40 | convolution fusion | flops 405012480 | bytes 5325568 | tf_op jit(solution)/shard_map/sxyk,kz->sxyz/dot_general | solution.py:22
  (91 shorter events, 176.0 us)
Async XLA Ops:
  0.0 343.1 %copy-start = (f32[8,8]{1,0:T(8,128)S(1)}, f32[8,8]{1,0:T(8,128)}, u32[]{:S(2)}) copy-start(f32[8,8]{1,0:T(8,128)} %param.5) | copy-start | bytes 772
  0.0 2.7 copy-start.2
  0.3 2.5 copy-start.8
  0.5 5.6 copy-start.10
  2.7 3.5 copy-start.3
  42.0 59.9 %all-to-all-start = ((f32[4,1,262144]{2,1,0:T(1,128)}), f32[4,1,262144]{2,1,0:T(1,128)}, u32[]{:S(2)}, u32[]{:S(2)}) async-start(f32[4,1,262144]{2,1,0:T(1,128)} %reshape.175), calls=%async_computation | async-start | bytes 8388608 | tf_op jit(solution)/shard_map/all_to_all | solution.py:57
  166.9 3.9 copy-start.1
  338.0 5.9 copy-start.12
  338.0 104.5 %all-to-all-start.2 = ((f32[4,1,278528]{2,1,0:T(1,128)}), f32[4,1,278528]{2,1,0:T(1,128)}, u32[]{:S(2)}, u32[]{:S(2)}) async-start(f32[4,1,278528]{2,1,0:T(1,128)} %reshape.179), calls=%async_computation.2 | async-start | bytes 8912896 | tf_op jit(solution)/shard_map/all_to_all | solution.py:70
  532.4 5.0 copy-start.4
  532.4 5.0 copy-start.5
  540.5 3.1 copy-start.7
  544.1 3.6 copy-start.6
  709.3 29.1 %all-to-all-start.5 = ((f32[4,1,131072]{2,1,0:T(1,128)}), f32[4,1,131072]{2,1,0:T(1,128)}, u32[]{:S(2)}, u32[]{:S(2)}) async-start(f32[4,1,131072]{2,1,0:T(1,128)} %reshape.183), calls=%async_computation.5 | async-start | bytes 4194304 | tf_op jit(solution)/shard_map/all_to_all | solution.py:103
  764.0 4.4 copy-start.11
  768.3 6.8 copy-start.9
where the time goes:
time: 795 us; the launch traced here: 784 us
  local copies, waits for them, and re-layouts  354 us (45%)
  waiting for transfers between devices  121 us (15%)
  blocking collectives  109 us (14%)
  matrix products  105 us (13%)
  other arithmetic  78.8 us (10%)
  starting transfers between devices  14.7 us (2%)
    unnamed x36, local copies, waits for them, and re-layouts  135 us
    dot_general x21, matrix products, contract(): return jnp.einsum(form, values, table, precision=lax.Precision.HIGHEST)  102 us
    all_to_all x1, waiting for transfers between devices, per_device(): lax.all_to_all(lax.all_to_all(spectrum, 'sp', split_axis=4, concat_axis=2...  96.4 us
    all_to_all x1, blocking collectives, per_device(): lax.all_to_all(lax.all_to_all(new_hat, 'sp', split_axis=1, concat_axis=3,...  55 us
    all_to_all x3, local copies, waits for them, and re-layouts, per_device(): lax.all_to_all(spectrum, 'sp', split_axis=4, concat_axis=2, tiled=True)  46.4 us
    squeeze x4, local copies, waits for them, and re-layouts, rotate(): real_part, imag_part = (spectrum[0], spectrum[1])  37.2 us
    all_gather x1, blocking collectives, per_device(): highest = lax.all_gather(highest, 'pz', axis=3, tiled=True)  36.4 us
    all_to_all x3, local copies, waits for them, and re-layouts, per_device(): lax.all_to_all(spectrum, 'pz', split_axis=5, concat_axis=4, tiled=True)  35.2 us
  transfers between devices with their start and end apart: 3, of which 2 were waited for; matrix products, arithmetic and copies ran while one was open for 3% of the time, Pallas kernels for 0%

commit v1 on v0

--- a/solution.py
+++ b/solution.py
@@ -1,8 +1,12 @@
+import functools
 import math
 
 import jax
 import jax.numpy as jnp
+import numpy as np
 from jax import lax
+from jax.experimental import pallas as pl
+from jax.experimental.pallas import tpu as pltpu
 from jax.sharding import PartitionSpec as P
 
 
@@ -34,7 +38,7 @@
     return jnp.stack([real_cos - imag_sin, imag_cos + real_sin])
 
 
-def per_device(concentration, mobility, kappa, well_depth):
+def per_device_general(concentration, mobility, kappa, well_depth):
     local_species, rows_x, rows_y, depth = concentration.shape
     count_sp = lax.axis_size("sp")
     count_py = lax.axis_size("py")
@@ -110,6 +114,343 @@
     return result * (1.0 / (full_x * full_y * depth))
 
 
+def basis(count):
+    grid = np.arange(count)
+    mode = np.arange(count)
+    freq = np.minimum(mode, count - mode)
+    angle = 2.0 * np.pi * (grid[:, None] * freq[None, :] % count) / count
+    table = np.where(mode[None, :] <= count // 2, np.cos(angle), np.sin(angle))
+    single = (mode == 0) | (2 * mode == count)
+    return table * np.sqrt(np.where(single, 1.0, 2.0) / count)[None, :]
+
+
+def split_table(table):
+    table = table.astype(np.float32)
+    high = table.astype(jnp.bfloat16)
+    low = (table - high.astype(np.float32)).astype(jnp.bfloat16)
+    row = np.concatenate([high, low], axis=1)
+    return np.concatenate([row, row], axis=0)
+
+
+def split(values, axis):
+    high = values.astype(jnp.bfloat16)
+    low = (values - high.astype(jnp.float32)).astype(jnp.bfloat16)
+    return jnp.concatenate([high, low], axis=axis)
+
+
+def from_right(values, table):
+    count = values.shape[1]
+    out = jnp.dot(split(values, 1), table, preferred_element_type=jnp.float32)
+    return out[:, :count] + out[:, count:]
+
+
+def from_left(table, values):
+    count = values.shape[0]
+    out = jnp.dot(table, split(values, 0), preferred_element_type=jnp.float32)
+    return out[:count] + out[count:]
+
+
+def swap_blocks(parts, width):
+    parts = list(parts)
+    axis = parts[0].ndim - 1
+    lanes = parts[0].shape[axis]
+    block = lax.broadcasted_iota(jnp.int32, parts[0].shape, axis) // width
+    half = len(parts) // 2
+    while half:
+        low_side = (block // half) % 2 == 0
+        for first in range(len(parts)):
+            if (first // half) % 2 == 0:
+                one, two = parts[first], parts[first + half]
+                parts[first] = jnp.where(low_side, one, pltpu.roll(two, half * width, axis))
+                parts[first + half] = jnp.where(
+                    low_side, pltpu.roll(one, lanes - half * width, axis), two
+                )
+        half //= 2
+    return parts
+
+
+def kernel(
+    sizes, conc, mobility, kappa, depths, right_f, right_i, left_f, left_i, out,
+    other, other_depths, z_out, z_in, y_out, y_in, x_out, x_in, w_out, w_in,
+    pair_send, pair_recv, zs, zr, ys, yr, xs, xr, ws, wr,
+):
+    count_py, count_pz = sizes
+    species, rows_x, rows_y, n = conc.shape
+    me_sp, me_py, me_pz = lax.axis_index("sp"), lax.axis_index("py"), lax.axis_index("pz")
+    width = n // count_pz
+    groups = rows_x // count_pz
+    own_ky = n // count_py
+    sub = own_ky // count_pz
+    strip = rows_x * sub
+    mesh_id = pl.DeviceIdType.MESH
+
+    def along_py(step):
+        return {"sp": me_sp, "py": lax.rem(me_py + step, count_py), "pz": me_pz}
+
+    def along_pz(step):
+        return {"sp": me_sp, "py": me_py, "pz": lax.rem(me_pz + step, count_pz)}
+
+    partner = {"sp": 1 - me_sp, "py": me_py, "pz": me_pz}
+    barrier = pltpu.get_barrier_semaphore()
+    peers = [partner]
+    peers += [along_pz(step) for step in range(1, count_pz)]
+    peers += [along_py(step) for step in range(1, count_py)]
+    for peer in peers:
+        pl.semaphore_signal(barrier, inc=1, device_id=peer, device_id_type=mesh_id)
+    pl.semaphore_wait(barrier, len(peers))
+
+    def remote(source, target, send, recv, peer):
+        return pltpu.make_async_remote_copy(
+            src_ref=source, dst_ref=target, send_sem=send, recv_sem=recv,
+            device_id=peer, device_id_type=mesh_id,
+        )
+
+    pair = [
+        remote(depths, other_depths, pair_send.at[0], pair_recv.at[0], partner),
+        remote(conc, other, pair_send.at[1], pair_recv.at[1], partner),
+    ]
+    for copy in pair:
+        copy.start()
+
+    y_rows = pl.ds(pl.multiple_of(me_pz * rows_y, rows_y), rows_y)
+    x_rows = pl.ds(pl.multiple_of(me_py * strip, strip), strip)
+
+    def z_copy(chunk, step):
+        peer = lax.rem(me_pz + step, count_pz)
+        return remote(
+            z_out.at[chunk, peer], z_in.at[chunk, :, y_rows], zs.at[chunk, step],
+            zr.at[chunk, step], along_pz(step),
+        )
+
+    def y_copy(chunk, step):
+        peer = lax.rem(me_py + step, count_py)
+        return remote(
+            y_out.at[chunk, peer], y_in.at[chunk, x_rows], ys.at[chunk, step],
+            yr.at[chunk, step], along_py(step),
+        )
+
+    def x_copy(one, step):
+        peer = lax.rem(me_py + step, count_py)
+        rows = pl.ds(pl.multiple_of(peer * strip, strip), strip)
+        return remote(
+            x_out.at[one, rows], x_in.at[one, me_py], xs.at[one, step],
+            xr.at[one, step], along_py(step),
+        )
+
+    def w_copy(one, step):
+        peer = lax.rem(me_pz + step, count_pz)
+        return remote(
+            w_out.at[one, peer], w_in.at[one, me_pz], ws.at[one, step],
+            wr.at[one, step], along_pz(step),
+        )
+
+    for copy in pair:
+        copy.wait_recv()
+
+    def z_forward(one, _):
+        own_i = me_sp * species + one
+        terms = []
+        for side, field, depth in ((me_sp, conc, depths), (1 - me_sp, other, other_depths)):
+            for t in range(species):
+                j = side * species + t
+                weight = mobility[own_i, j]
+                terms.append((field, t, weight * depth[t : t + 1, :], weight * kappa[j]))
+        for g in range(groups):
+            bulk_mix, conc_mix = [], []
+            for block in range(count_pz):
+                first = second = None
+                for field, t, bulk_weight, conc_weight in terms:
+                    c = field[t, block * groups + g]
+                    a = bulk_weight * (c * c * c - c)
+                    b = conc_weight * c
+                    first = a if first is None else first + a
+                    second = b if second is None else second + b
+                bulk_mix.append(first)
+                conc_mix.append(second)
+            modes = from_right(jnp.concatenate(bulk_mix + conc_mix, axis=0), right_f[...])
+            modes = modes.reshape(2, count_pz, rows_y, n)
+            for f in range(2):
+                swapped = swap_blocks([modes[f, block] for block in range(count_pz)], width)
+                for q in range(count_pz):
+                    z_out[2 * one + f, q, g] = swapped[q]
+        for f in range(2):
+            for step in range(1, count_pz):
+                z_copy(2 * one + f, step).start()
+        for f in range(2):
+            z_in[2 * one + f, :, y_rows] = z_out[2 * one + f, me_pz]
+        return 0
+
+    lax.fori_loop(0, species, z_forward, 0)
+
+    def y_forward(chunk, _):
+        for step in range(1, count_pz):
+            z_copy(chunk, step).wait_recv()
+        for g in range(0, groups, 2):
+            lines = jnp.concatenate([z_in[chunk, g], z_in[chunk, g + 1]], axis=1)
+            modes = from_left(left_f[...], lines)
+            for h in range(2):
+                part = modes[:, h * n : (h + 1) * n].reshape(count_py, count_pz, sub, n)
+                swapped = swap_blocks([part[:, b] for b in range(count_pz)], width)
+                for block in range(count_pz):
+                    start = (block * groups + g + h) * sub
+                    y_out[chunk, :, start : start + sub, :] = swapped[block]
+        for step in range(1, count_py):
+            y_copy(chunk, step).start()
+        y_in[chunk, x_rows] = y_out[chunk, me_py]
+        return 0
+
+    lax.fori_loop(0, 2 * species, y_forward, 0)
+
+    def square(index):
+        freq = jnp.minimum(index, n - index).astype(jnp.float32)
+        root = freq * (2.0 * math.pi / n)
+        return root * root
+
+    lane = lax.broadcasted_iota(jnp.int32, (1, n), 1)
+    ksq_x = square(lax.broadcasted_iota(jnp.int32, (n, 1), 0))
+    ksq_z = square(me_pz * width + lane % width)
+
+    def x_both(one, _):
+        for f in range(2):
+            for step in range(1, count_py):
+                y_copy(2 * one + f, step).wait_recv()
+        own_i = me_sp * species + one
+        half_stiff = 0.5 * (mobility[own_i, own_i] * kappa[own_i])
+        for r in range(0, sub, 2):
+            both, ksq = [], []
+            for f in range(2):
+                both.append(from_left(left_f[...], jnp.concatenate(
+                    [y_in[2 * one + f, pl.ds(r + h, n, stride=sub), :] for h in range(2)], axis=1
+                )))
+            for h in range(2):
+                ksq_y = square(me_py * own_ky + (lane // width) * sub + (r + h))
+                ksq.append(ksq_x + (ksq_y + ksq_z))
+            ksq = jnp.concatenate(ksq, axis=1)
+            drop = 0.5 * ksq * (both[0] + ksq * both[1]) / (1.0 + half_stiff * (ksq * ksq))
+            lines = from_left(left_i[...], drop)
+            for h in range(2):
+                x_out[one, pl.ds(r + h, n, stride=sub), :] = lines[:, h * n : (h + 1) * n]
+        for step in range(1, count_py):
+            x_copy(one, step).start()
+        x_in[one, me_py] = x_out[one, x_rows]
+        return 0
+
+    lax.fori_loop(0, species, x_both, 0)
+
+    def y_back(one, _):
+        for step in range(1, count_py):
+            x_copy(one, step).wait_recv()
+        for g in range(0, groups, 2):
+            pairs = []
+            for h in range(2):
+                parts = []
+                for block in range(count_pz):
+                    start = (block * groups + g + h) * sub
+                    parts.append(x_in[one, :, start : start + sub, :])
+                swapped = swap_blocks(parts, width)
+                pairs.append(jnp.stack(swapped, axis=1).reshape(n, n))
+            lines = from_left(left_i[...], jnp.concatenate(pairs, axis=1))
+            for h in range(2):
+                part = lines[:, h * n : (h + 1) * n].reshape(count_pz, rows_y, n)
+                w_out[one, :, g + h] = part
+        for step in range(1, count_pz):
+            w_copy(one, step).start()
+        w_in[one, me_pz] = w_out[one, me_pz]
+        return 0
+
+    lax.fori_loop(0, species, y_back, 0)
+
+    def z_back(one, _):
+        for step in range(1, count_pz):
+            w_copy(one, step).wait_recv()
+        for g in range(0, groups, 2):
+            rows = []
+            for h in range(2):
+                rows += swap_blocks([w_in[one, q, g + h] for q in range(count_pz)], width)
+            lines = from_right(jnp.concatenate(rows, axis=0), right_i[...])
+            lines = lines.reshape(2, count_pz, rows_y, n)
+            for h in range(2):
+                for block in range(count_pz):
+                    x = block * groups + g + h
+                    out[one, x] = conc[one, x] - lines[h, block]
+        return 0
+
+    lax.fori_loop(0, species, z_back, 0)
+
+    for copy in pair:
+        copy.wait_send()
+
+    def drain(one, _):
+        for step in range(1, count_pz):
+            z_copy(2 * one, step).wait_send()
+            z_copy(2 * one + 1, step).wait_send()
+            w_copy(one, step).wait_send()
+        for step in range(1, count_py):
+            y_copy(2 * one, step).wait_send()
+            y_copy(2 * one + 1, step).wait_send()
+            x_copy(one, step).wait_send()
+        return 0
+
+    lax.fori_loop(0, species, drain, 0)
+
+
+def per_device_kernel(concentration, mobility, kappa, well_depth):
+    species, rows_x, rows_y, n = concentration.shape
+    count_py, count_pz = lax.axis_size("py"), lax.axis_size("pz")
+    forward = split_table(basis(n))
+    inverse = split_table(basis(n).T)
+    depths = jnp.broadcast_to(well_depth[:, None], (species, n))
+    groups = rows_x // count_pz
+    sub = n // count_py // count_pz
+    strip = rows_x * sub
+    f32 = jnp.float32
+    vmem = pl.BlockSpec(memory_space=pltpu.VMEM)
+    smem = pl.BlockSpec(memory_space=pltpu.SMEM)
+    dma = pltpu.SemaphoreType.DMA
+    return pl.pallas_call(
+        functools.partial(kernel, (count_py, count_pz)),
+        out_shape=jax.ShapeDtypeStruct(concentration.shape, f32),
+        in_specs=[vmem, smem, smem, vmem, vmem, vmem, vmem, vmem],
+        out_specs=vmem,
+        scratch_shapes=[
+            pltpu.VMEM((species, rows_x, rows_y, n), f32),
+            pltpu.VMEM((species, n), f32),
+            pltpu.VMEM((2 * species, count_pz, groups, rows_y, n), f32),
+            pltpu.VMEM((2 * species, groups, n, n), f32),
+            pltpu.VMEM((2 * species, count_py, strip, n), f32),
+            pltpu.VMEM((2 * species, n * sub, n), f32),
+            pltpu.VMEM((species, n * sub, n), f32),
+            pltpu.VMEM((species, count_py, strip, n), f32),
+            pltpu.VMEM((species, count_pz, groups, rows_y, n), f32),
+            pltpu.VMEM((species, count_pz, groups, rows_y, n), f32),
+            dma((2,)), dma((2,)),
+            dma((2 * species, count_pz)), dma((2 * species, count_pz)),
+            dma((2 * species, count_py)), dma((2 * species, count_py)),
+            dma((species, count_py)), dma((species, count_py)),
+            dma((species, count_pz)), dma((species, count_pz)),
+        ],
+        compiler_params=pltpu.CompilerParams(
+            collective_id=0, has_side_effects=True, vmem_limit_bytes=60 * 1024 * 1024
+        ),
+        name="step",
+    )(
+        concentration, mobility, kappa, depths,
+        jnp.asarray(forward), jnp.asarray(inverse),
+        jnp.asarray(forward.T), jnp.asarray(inverse.T),
+    )
+
+
+def per_device(concentration, mobility, kappa, well_depth):
+    rows_x, rows_y, n = concentration.shape[1:]
+    count_sp, count_py, count_pz = (lax.axis_size(name) for name in ("sp", "py", "pz"))
+    cube = rows_x * count_py == n and rows_y * count_pz == n and n == 128
+    power = count_pz > 1 and count_pz & (count_pz - 1) == 0
+    whole = n % (8 * count_py * count_pz) == 0 and rows_x % (2 * count_pz) == 0 and rows_y % 8 == 0
+    if cube and power and whole and count_sp == 2:
+        return per_device_kernel(concentration, mobility, kappa, well_depth)
+    return per_device_general(concentration, mobility, kappa, well_depth)
+
+
 def solution(mesh):
     in_specs = (P("sp", "py", "pz", None), P(), P(), P("sp"))
     out_specs = P("sp", "py", "pz", None)

time: 795 us -> 172 us (0.22); the launches traced: 784 us -> 172 us
  local copies, waits for them, and re-layouts: 354 us -> 4.38 us
  Pallas kernels: 0 us -> 167 us
  waiting for transfers between devices: 121 us -> 0 us
  blocking collectives: 109 us -> 0 us
  matrix products: 105 us -> 0 us
  other arithmetic: 78.8 us -> 0 us
  starting transfers between devices: 14.7 us -> 0 us
    pallas_call x0 -> x1, Pallas kernels: none -> 167 us  [per_device_kernel(): pl.pallas_call(functools.partial(kernel, (count_py, count_pz)), out_shape...]
    unnamed x36 -> x1, local copies, waits for them, and re-layouts: 135 us -> 3.08 us
    all_to_all x11 -> x0, local copies, waits for them, and re-layouts: 122 us -> none  [the longest x3 46.4 us: per_device(): lax.all_to_all(spectrum, 'sp', split_axis=4, concat_axis=2, tiled=True)]
    all_to_all x3 -> x0, waiting for transfers between devices: 121 us -> none  [the longest x1 96.4 us: per_device(): lax.all_to_all(lax.all_to_all(spectrum, 'sp', split_axis=4, concat_axis=2...]
    dot_general x22 -> x0, matrix products: 105 us -> none  [the longest x21 102 us: contract(): return jnp.einsum(form, values, table, precision=lax.Precision.HIGHEST)]
    all_to_all x3 -> x0, blocking collectives: 73 us -> none  [the longest x1 55 us: per_device(): lax.all_to_all(lax.all_to_all(new_hat, 'sp', split_axis=1, concat_axis=3,...]
    all_to_all x5 -> x0, other arithmetic: 64.9 us -> none  [the longest x1 17.5 us: per_device(): lax.all_to_all(spectrum, 'sp', split_axis=4, concat_axis=2, tiled=True)]
    squeeze x4 -> x0, local copies, waits for them, and re-layouts: 37.2 us -> none  [rotate(): real_part, imag_part = (spectrum[0], spectrum[1])]
  transfers between devices with their start and end apart: 3 -> 0, of which waited for: 2 -> 0; matrix products, arithmetic and copies ran while one was open for 3% -> 0% of each run, Pallas kernels for 0% -> 0%
where the time goes in v1:
time: 172 us
  Pallas kernels  167 us (97%)
  local copies, waits for them, and re-layouts  4.38 us (3%)
    pallas_call x1, Pallas kernels, per_device_kernel(): pl.pallas_call(functools.partial(kernel, (count_py, count_pz)), out_shape...  167 us

profile of v1, /device:TPU:0, one launch (start us, length us, event | category | flops | bytes accessed | tf_op | source)
XLA Modules:
  0.0 171.6 jit_solution(16961469256429053)
XLA Ops:
  0.0 1.3 broadcast_in_dim.2.depths
  1.3 167.2 %step.1 = f32[4,32,32,128]{3,2,1,0:T(8,128)} custom-call(f32[4,32,32,128]{3,2,1,0:T(8,128)} %conc.1, f32[8,8]{1,0:T(8,128)} %mobility.1, f32[8]{0:T(128)} %kappa.1, f32[4,128]{1,0:T(4,128)} %broadcast_in_dim.2.depths, bf16[256,256]{1,0:T(8,128)(2,1)} %constant.8.clone.right_f, bf16[256,256]{1,0:T(8,128)(2,1)} %constant.9.clone.right_i, ...), custom_call_target="tpu_custom_call" | custom-call | tf_op jit(solution)/shard_map/step/pallas_call | solution.py:410
  168.5 3.1 %copy.10 = f32[4,32,32,128]{3,2,1,0:T(8,128)} copy(f32[4,32,32,128]{3,2,1,0:T(8,128)} %step.1) | data formatting | bytes 4194304

commit v2 on v1

--- a/solution.py
+++ b/solution.py
@@ -145,7 +145,7 @@
 
 
 def from_left(table, values):
-    count = values.shape[0]
+    count = table.shape[0] // 2
     out = jnp.dot(table, split(values, 0), preferred_element_type=jnp.float32)
     return out[:count] + out[count:]
 
@@ -170,31 +170,34 @@
 
 
 def kernel(
-    sizes, conc, mobility, kappa, depths, right_f, right_i, left_f, left_i, out,
-    other, other_depths, z_out, z_in, y_out, y_in, x_out, x_in, w_out, w_in,
-    pair_send, pair_recv, zs, zr, ys, yr, xs, xr, ws, wr,
+    sizes, conc, mobility, kappa, depths, right_f, right_i, left_f, left_i, half_f, half_i, out,
+    other, other_depths, z_out, z_in, y_out, y_in, near, x_out, x_in, b_out, b_in, w_out, w_in,
+    pair_send, pair_recv, zs, zr, ys, yr, xs, xr, bs, br, ws, wr,
 ):
     count_py, count_pz = sizes
     species, rows_x, rows_y, n = conc.shape
     me_sp, me_py, me_pz = lax.axis_index("sp"), lax.axis_index("py"), lax.axis_index("pz")
     width = n // count_pz
     groups = rows_x // count_pz
-    own_ky = n // count_py
-    sub = own_ky // count_pz
+    slabs = count_py
+    slab_ky = n // slabs
+    sub = slab_ky // count_pz
     strip = rows_x * sub
     mesh_id = pl.DeviceIdType.MESH
 
-    def along_py(step):
-        return {"sp": me_sp, "py": lax.rem(me_py + step, count_py), "pz": me_pz}
+    half = me_py // 2
+    inner = lax.rem(me_py + half, 2) == 1
+    outer = jnp.logical_not(inner)
+    buddy = {"sp": me_sp, "py": me_py + 1 - 2 * lax.rem(me_py, 2), "pz": me_pz}
+    across = {"sp": me_sp, "py": count_py - 1 - me_py, "pz": me_pz}
 
     def along_pz(step):
         return {"sp": me_sp, "py": me_py, "pz": lax.rem(me_pz + step, count_pz)}
 
     partner = {"sp": 1 - me_sp, "py": me_py, "pz": me_pz}
     barrier = pltpu.get_barrier_semaphore()
-    peers = [partner]
+    peers = [partner, buddy, across]
     peers += [along_pz(step) for step in range(1, count_pz)]
-    peers += [along_py(step) for step in range(1, count_py)]
     for peer in peers:
         pl.semaphore_signal(barrier, inc=1, device_id=peer, device_id_type=mesh_id)
     pl.semaphore_wait(barrier, len(peers))
@@ -213,7 +216,6 @@
         copy.start()
 
     y_rows = pl.ds(pl.multiple_of(me_pz * rows_y, rows_y), rows_y)
-    x_rows = pl.ds(pl.multiple_of(me_py * strip, strip), strip)
 
     def z_copy(chunk, step):
         peer = lax.rem(me_pz + step, count_pz)
@@ -222,19 +224,20 @@
             zr.at[chunk, step], along_pz(step),
         )
 
-    def y_copy(chunk, step):
-        peer = lax.rem(me_py + step, count_py)
+    def y_copy(chunk, slab):
         return remote(
-            y_out.at[chunk, peer], y_in.at[chunk, x_rows], ys.at[chunk, step],
-            yr.at[chunk, step], along_py(step),
+            y_out.at[chunk, slab], y_in.at[chunk, slab], ys.at[chunk, slab],
+            yr.at[chunk, slab], buddy,
         )
 
-    def x_copy(one, step):
-        peer = lax.rem(me_py + step, count_py)
-        rows = pl.ds(pl.multiple_of(peer * strip, strip), strip)
+    def x_copy(one, slab):
         return remote(
-            x_out.at[one, rows], x_in.at[one, me_py], xs.at[one, step],
-            xr.at[one, step], along_py(step),
+            x_out.at[one, slab], x_in.at[one, slab], xs.at[one, slab], xr.at[one, slab], across
+        )
+
+    def b_copy(one, slab):
+        return remote(
+            b_out.at[one, slab], b_in.at[one, slab], bs.at[one, slab], br.at[one, slab], buddy
         )
 
     def w_copy(one, step):
@@ -247,7 +250,7 @@
     for copy in pair:
         copy.wait_recv()
 
-    def z_forward(one, _):
+    def z_forward(one):
         own_i = me_sp * species + one
         terms = []
         for side, field, depth in ((me_sp, conc, depths), (1 - me_sp, other, other_depths)):
@@ -278,28 +281,29 @@
                 z_copy(2 * one + f, step).start()
         for f in range(2):
             z_in[2 * one + f, :, y_rows] = z_out[2 * one + f, me_pz]
-        return 0
-
-    lax.fori_loop(0, species, z_forward, 0)
-
-    def y_forward(chunk, _):
+
+    def y_chunk(chunk, _):
         for step in range(1, count_pz):
             z_copy(chunk, step).wait_recv()
         for g in range(0, groups, 2):
             lines = jnp.concatenate([z_in[chunk, g], z_in[chunk, g + 1]], axis=1)
             modes = from_left(left_f[...], lines)
             for h in range(2):
-                part = modes[:, h * n : (h + 1) * n].reshape(count_py, count_pz, sub, n)
+                part = modes[:, h * n : (h + 1) * n].reshape(slabs, count_pz, sub, n)
                 swapped = swap_blocks([part[:, b] for b in range(count_pz)], width)
                 for block in range(count_pz):
                     start = (block * groups + g + h) * sub
                     y_out[chunk, :, start : start + sub, :] = swapped[block]
-        for step in range(1, count_py):
-            y_copy(chunk, step).start()
-        y_in[chunk, x_rows] = y_out[chunk, me_py]
         return 0
 
-    lax.fori_loop(0, 2 * species, y_forward, 0)
+    def y_forward(one):
+        lax.fori_loop(2 * one, 2 * one + 2, y_chunk, 0)
+
+        @pl.when(outer)
+        def _():
+            for slab in range(slabs):
+                for f in range(2):
+                    y_copy(2 * one + f, slab).start()
 
     def square(index):
         freq = jnp.minimum(index, n - index).astype(jnp.float32)
@@ -310,43 +314,53 @@
     ksq_x = square(lax.broadcasted_iota(jnp.int32, (n, 1), 0))
     ksq_z = square(me_pz * width + lane % width)
 
-    def x_both(one, _):
+    def x_both(one, slab):
         for f in range(2):
-            for step in range(1, count_py):
-                y_copy(2 * one + f, step).wait_recv()
+            y_copy(2 * one + f, slab).wait_recv()
         own_i = me_sp * species + one
         half_stiff = 0.5 * (mobility[own_i, own_i] * kappa[own_i])
         for r in range(0, sub, 2):
             both, ksq = [], []
             for f in range(2):
-                both.append(from_left(left_f[...], jnp.concatenate(
-                    [y_in[2 * one + f, pl.ds(r + h, n, stride=sub), :] for h in range(2)], axis=1
-                )))
-            for h in range(2):
-                ksq_y = square(me_py * own_ky + (lane // width) * sub + (r + h))
+                chunk = 2 * one + f
+                both.append(from_left(half_f[half], jnp.concatenate([
+                    jnp.concatenate([
+                        field[chunk, slab, pl.ds(r + h, rows_x, stride=sub), :]
+                        for field in (y_out, y_in)
+                    ], axis=0)
+                    for h in range(2)
+                ], axis=1)))
+            for h in range(2):
+                ksq_y = square(slab * slab_ky + (lane // width) * sub + (r + h))
                 ksq.append(ksq_x + (ksq_y + ksq_z))
             ksq = jnp.concatenate(ksq, axis=1)
             drop = 0.5 * ksq * (both[0] + ksq * both[1]) / (1.0 + half_stiff * (ksq * ksq))
-            lines = from_left(left_i[...], drop)
-            for h in range(2):
-                x_out[one, pl.ds(r + h, n, stride=sub), :] = lines[:, h * n : (h + 1) * n]
-        for step in range(1, count_py):
-            x_copy(one, step).start()
-        x_in[one, me_py] = x_out[one, x_rows]
-        return 0
-
-    lax.fori_loop(0, species, x_both, 0)
-
-    def y_back(one, _):
-        for step in range(1, count_py):
-            x_copy(one, step).wait_recv()
+            lines = from_left(half_i[half], drop)
+            for h in range(2):
+                rows = pl.ds(r + h, n // 2, stride=sub)
+                near[one, slab, rows, :] = lines[: n // 2, h * n : (h + 1) * n]
+                x_out[one, slab, rows, :] = lines[n // 2 :, h * n : (h + 1) * n]
+        x_copy(one, slab).start()
+
+    def combine(one, slab):
+        x_copy(one, slab).wait_recv()
+        b_out[one, slab] = near[one, slab, strip:, :] + x_in[one, slab, strip:, :]
+        b_copy(one, slab).start()
+        b_in[one, slab] = near[one, slab, :strip, :] + x_in[one, slab, :strip, :]
+
+    def y_back(one):
+        @pl.when(outer)
+        def _():
+            for slab in range(slabs):
+                b_copy(one, slab).wait_recv()
+
         for g in range(0, groups, 2):
             pairs = []
             for h in range(2):
                 parts = []
                 for block in range(count_pz):
                     start = (block * groups + g + h) * sub
-                    parts.append(x_in[one, :, start : start + sub, :])
+                    parts.append(b_in[one, :, start : start + sub, :])
                 swapped = swap_blocks(parts, width)
                 pairs.append(jnp.stack(swapped, axis=1).reshape(n, n))
             lines = from_left(left_i[...], jnp.concatenate(pairs, axis=1))
@@ -356,11 +370,8 @@
         for step in range(1, count_pz):
             w_copy(one, step).start()
         w_in[one, me_pz] = w_out[one, me_pz]
-        return 0
-
-    lax.fori_loop(0, species, y_back, 0)
-
-    def z_back(one, _):
+
+    def z_back(one):
         for step in range(1, count_pz):
             w_copy(one, step).wait_recv()
         for g in range(0, groups, 2):
@@ -373,9 +384,50 @@
                 for block in range(count_pz):
                     x = block * groups + g + h
                     out[one, x] = conc[one, x] - lines[h, block]
+
+    def opening(one, _):
+        z_forward(one)
+
+        @pl.when(jnp.logical_and(one >= 1, one <= 2))
+        def _():
+            y_forward(one - 1)
+
         return 0
 
-    lax.fori_loop(0, species, z_back, 0)
+    lax.fori_loop(0, species, opening, 0)
+    steps = species * slabs
+    lag = 2
+
+    def middle(k, _):
+        @pl.when(jnp.logical_and(inner, k < steps))
+        def _():
+            x_both(k // slabs, lax.rem(k, slabs))
+
+        later = k // slabs + 2
+
+        @pl.when(jnp.logical_and(lax.rem(k, slabs) == 1, later < species))
+        def _():
+            y_forward(later)
+
+        back = k - lag
+
+        @pl.when(jnp.logical_and(inner, jnp.logical_and(back >= 0, back < steps)))
+        def _():
+            combine(back // slabs, lax.rem(back, slabs))
+
+        last = jnp.logical_and(back >= 0, lax.rem(k + slabs - lag, slabs) == slabs - 1)
+
+        @pl.when(jnp.logical_and(last, back < steps))
+        def _():
+            y_back(back // slabs)
+
+        @pl.when(jnp.logical_and(last, back >= slabs))
+        def _():
+            z_back(back // slabs - 1)
+
+        return 0
+
+    lax.fori_loop(0, steps + slabs + lag, middle, 0)
 
     for copy in pair:
         copy.wait_send()
@@ -385,10 +437,19 @@
             z_copy(2 * one, step).wait_send()
             z_copy(2 * one + 1, step).wait_send()
             w_copy(one, step).wait_send()
-        for step in range(1, count_py):
-            y_copy(2 * one, step).wait_send()
-            y_copy(2 * one + 1, step).wait_send()
-            x_copy(one, step).wait_send()
+
+        @pl.when(outer)
+        def _():
+            for slab in range(slabs):
+                y_copy(2 * one, slab).wait_send()
+                y_copy(2 * one + 1, slab).wait_send()
+
+        @pl.when(inner)
+        def _():
+            for slab in range(slabs):
+                x_copy(one, slab).wait_send()
+                b_copy(one, slab).wait_send()
+
         return 0
 
     lax.fori_loop(0, species, drain, 0)
@@ -397,8 +458,13 @@
 def per_device_kernel(concentration, mobility, kappa, well_depth):
     species, rows_x, rows_y, n = concentration.shape
     count_py, count_pz = lax.axis_size("py"), lax.axis_size("pz")
-    forward = split_table(basis(n))
-    inverse = split_table(basis(n).T)
+    table = basis(n)
+    forward = split_table(table)
+    inverse = split_table(table.T)
+    blocks = np.arange(n).reshape(count_py, rows_x)
+    orders = [blocks[[1, 0, 2, 3]].reshape(n), blocks[[2, 3, 1, 0]].reshape(n)]
+    half_forward = np.stack([split_table(table[order[: n // 2]]).T for order in orders])
+    half_inverse = np.stack([split_table(table[order].T).T for order in orders])
     depths = jnp.broadcast_to(well_depth[:, None], (species, n))
     groups = rows_x // count_pz
     sub = n // count_py // count_pz
@@ -410,7 +476,7 @@
     return pl.pallas_call(
         functools.partial(kernel, (count_py, count_pz)),
         out_shape=jax.ShapeDtypeStruct(concentration.shape, f32),
-        in_specs=[vmem, smem, smem, vmem, vmem, vmem, vmem, vmem],
+        in_specs=[vmem, smem, smem] + [vmem] * 7,
         out_specs=vmem,
         scratch_shapes=[
             pltpu.VMEM((species, rows_x, rows_y, n), f32),
@@ -418,14 +484,18 @@
             pltpu.VMEM((2 * species, count_pz, groups, rows_y, n), f32),
             pltpu.VMEM((2 * species, groups, n, n), f32),
             pltpu.VMEM((2 * species, count_py, strip, n), f32),
-            pltpu.VMEM((2 * species, n * sub, n), f32),
-            pltpu.VMEM((species, n * sub, n), f32),
+            pltpu.VMEM((2 * species, count_py, strip, n), f32),
+            pltpu.VMEM((species, count_py, 2 * strip, n), f32),
+            pltpu.VMEM((species, count_py, 2 * strip, n), f32),
+            pltpu.VMEM((species, count_py, 2 * strip, n), f32),
+            pltpu.VMEM((species, count_py, strip, n), f32),
             pltpu.VMEM((species, count_py, strip, n), f32),
             pltpu.VMEM((species, count_pz, groups, rows_y, n), f32),
             pltpu.VMEM((species, count_pz, groups, rows_y, n), f32),
             dma((2,)), dma((2,)),
             dma((2 * species, count_pz)), dma((2 * species, count_pz)),
             dma((2 * species, count_py)), dma((2 * species, count_py)),
+            dma((species, count_py)), dma((species, count_py)),
             dma((species, count_py)), dma((species, count_py)),
             dma((species, count_pz)), dma((species, count_pz)),
         ],
@@ -437,6 +507,7 @@
         concentration, mobility, kappa, depths,
         jnp.asarray(forward), jnp.asarray(inverse),
         jnp.asarray(forward.T), jnp.asarray(inverse.T),
+        jnp.asarray(half_forward), jnp.asarray(half_inverse),
     )
 
 
@@ -446,7 +517,7 @@
     cube = rows_x * count_py == n and rows_y * count_pz == n and n == 128
     power = count_pz > 1 and count_pz & (count_pz - 1) == 0
     whole = n % (8 * count_py * count_pz) == 0 and rows_x % (2 * count_pz) == 0 and rows_y % 8 == 0
-    if cube and power and whole and count_sp == 2:
+    if cube and power and whole and count_sp == 2 and count_py == 4 and concentration.shape[0] > 3:
         return per_device_kernel(concentration, mobility, kappa, well_depth)
     return per_device_general(concentration, mobility, kappa, well_depth)
 

time: 172 us -> 153 us (0.89)
  Pallas kernels: 167 us -> 149 us
    pallas_call x1, Pallas kernels: 167 us -> 149 us  [per_device_kernel(): pl.pallas_call(functools.partial(kernel, (count_py, count_pz)), out_shape...]
where the time goes in v2:
time: 153 us
  Pallas kernels  149 us (97%)
  local copies, waits for them, and re-layouts  4.38 us (3%)
    pallas_call x1, Pallas kernels, per_device_kernel(): pl.pallas_call(functools.partial(kernel, (count_py, count_pz)), out_shape...  149 us
    unnamed x1, local copies, waits for them, and re-layouts  3.08 us

profile of v2, /device:TPU:0, one launch (start us, length us, event | category | flops | bytes accessed | tf_op | source)
XLA Modules:
  0.0 153.0 jit_solution(12724980699880692164)
XLA Ops:
  0.0 1.3 broadcast_in_dim.2.depths
  1.3 148.6 %step.1 = f32[4,32,32,128]{3,2,1,0:T(8,128)} custom-call(f32[4,32,32,128]{3,2,1,0:T(8,128)} %conc.1, f32[8,8]{1,0:T(8,128)} %mobility.1, f32[8]{0:T(128)} %kappa.1, f32[4,128]{1,0:T(4,128)} %broadcast_in_dim.2.depths, bf16[256,256]{1,0:T(8,128)(2,1)} %constant.12.clone.right_f, bf16[256,256]{1,0:T(8,128)(2,1)} %constant.13.clone.right_i, ...), custom_call_target="tpu_custom_call" | custom-call | tf_op jit(solution)/shard_map/step/pallas_call | solution.py:476
  149.9 3.1 %copy.12 = f32[4,32,32,128]{3,2,1,0:T(8,128)} copy(f32[4,32,32,128]{3,2,1,0:T(8,128)} %step.1) | data formatting | bytes 4194304

commit v3 on v2

--- a/solution.py
+++ b/solution.py
@@ -114,6 +114,10 @@
     return result * (1.0 / (full_x * full_y * depth))
 
 
+PIECES = 4
+SUBLANES = 8
+
+
 def basis(count):
     grid = np.arange(count)
     mode = np.arange(count)
@@ -170,18 +174,20 @@
 
 
 def kernel(
-    sizes, conc, mobility, kappa, depths, right_f, right_i, left_f, left_i, half_f, half_i, out,
-    other, other_depths, z_out, z_in, y_out, y_in, near, x_out, x_in, b_out, b_in, w_out, w_in,
+    sizes, conc, mobility, kappa, well_depth, right_f, right_i, left_f, left_i, half_f, half_i, out,
+    other, depths, other_depths, z_out, z_in, y_out, y_in, near, x_out, x_in, b_out, b_in, w_out, w_in,
     pair_send, pair_recv, zs, zr, ys, yr, xs, xr, bs, br, ws, wr,
 ):
     count_py, count_pz = sizes
     species, rows_x, rows_y, n = conc.shape
     me_sp, me_py, me_pz = lax.axis_index("sp"), lax.axis_index("py"), lax.axis_index("pz")
-    width = n // count_pz
-    groups = rows_x // count_pz
-    slabs = count_py
-    slab_ky = n // slabs
-    sub = slab_ky // count_pz
+    blocks = count_pz * PIECES
+    units = species * PIECES
+    width = n // blocks
+    groups = rows_x // blocks
+    sub = SUBLANES
+    slab_ky = blocks * sub
+    slabs = n // slab_ky
     strip = rows_x * sub
     mesh_id = pl.DeviceIdType.MESH
 
@@ -196,11 +202,18 @@
 
     partner = {"sp": 1 - me_sp, "py": me_py, "pz": me_pz}
     barrier = pltpu.get_barrier_semaphore()
-    peers = [partner, buddy, across]
+    peers = [partner, buddy]
     peers += [along_pz(step) for step in range(1, count_pz)]
     for peer in peers:
         pl.semaphore_signal(barrier, inc=1, device_id=peer, device_id_type=mesh_id)
-    pl.semaphore_wait(barrier, len(peers))
+
+    @pl.when(inner)
+    def _():
+        pl.semaphore_signal(barrier, inc=1, device_id=across, device_id_type=mesh_id)
+
+    for t in range(species):
+        depths[t : t + 1, :] = jnp.full((1, n), well_depth[t], jnp.float32)
+    pl.semaphore_wait(barrier, len(peers) + jnp.where(inner, 1, 0))
 
     def remote(source, target, send, recv, peer):
         return pltpu.make_async_remote_copy(
@@ -260,7 +273,7 @@
                 terms.append((field, t, weight * depth[t : t + 1, :], weight * kappa[j]))
         for g in range(groups):
             bulk_mix, conc_mix = [], []
-            for block in range(count_pz):
+            for block in range(blocks):
                 first = second = None
                 for field, t, bulk_weight, conc_weight in terms:
                     c = field[t, block * groups + g]
@@ -271,16 +284,18 @@
                 bulk_mix.append(first)
                 conc_mix.append(second)
             modes = from_right(jnp.concatenate(bulk_mix + conc_mix, axis=0), right_f[...])
-            modes = modes.reshape(2, count_pz, rows_y, n)
+            modes = modes.reshape(2, blocks, rows_y, n)
             for f in range(2):
-                swapped = swap_blocks([modes[f, block] for block in range(count_pz)], width)
-                for q in range(count_pz):
-                    z_out[2 * one + f, q, g] = swapped[q]
-        for f in range(2):
+                swapped = swap_blocks([modes[f, block] for block in range(blocks)], width)
+                for block in range(blocks):
+                    unit = PIECES * one + block % PIECES
+                    z_out[2 * unit + f, block // PIECES, g] = swapped[block]
+        for c in range(2 * PIECES):
             for step in range(1, count_pz):
-                z_copy(2 * one + f, step).start()
-        for f in range(2):
-            z_in[2 * one + f, :, y_rows] = z_out[2 * one + f, me_pz]
+                z_copy(2 * PIECES * one + c, step).start()
+        for c in range(2 * PIECES):
+            chunk = 2 * PIECES * one + c
+            z_in[chunk, :, y_rows] = z_out[chunk, me_pz]
 
     def y_chunk(chunk, _):
         for step in range(1, count_pz):
@@ -289,9 +304,9 @@
             lines = jnp.concatenate([z_in[chunk, g], z_in[chunk, g + 1]], axis=1)
             modes = from_left(left_f[...], lines)
             for h in range(2):
-                part = modes[:, h * n : (h + 1) * n].reshape(slabs, count_pz, sub, n)
-                swapped = swap_blocks([part[:, b] for b in range(count_pz)], width)
-                for block in range(count_pz):
+                part = modes[:, h * n : (h + 1) * n].reshape(slabs, blocks, sub, n)
+                swapped = swap_blocks([part[:, b] for b in range(blocks)], width)
+                for block in range(blocks):
                     start = (block * groups + g + h) * sub
                     y_out[chunk, :, start : start + sub, :] = swapped[block]
         return 0
@@ -312,12 +327,13 @@
 
     lane = lax.broadcasted_iota(jnp.int32, (1, n), 1)
     ksq_x = square(lax.broadcasted_iota(jnp.int32, (n, 1), 0))
-    ksq_z = square(me_pz * width + lane % width)
 
     def x_both(one, slab):
         for f in range(2):
             y_copy(2 * one + f, slab).wait_recv()
-        own_i = me_sp * species + one
+        own_i = me_sp * species + one // PIECES
+        piece = me_pz * PIECES + lax.rem(one, PIECES)
+        ksq_z = square(piece * width + lane % width)
         half_stiff = 0.5 * (mobility[own_i, own_i] * kappa[own_i])
         for r in range(0, sub, 2):
             both, ksq = [], []
@@ -358,7 +374,7 @@
             pairs = []
             for h in range(2):
                 parts = []
-                for block in range(count_pz):
+                for block in range(blocks):
                     start = (block * groups + g + h) * sub
                     parts.append(b_in[one, :, start : start + sub, :])
                 swapped = swap_blocks(parts, width)
@@ -372,30 +388,33 @@
         w_in[one, me_pz] = w_out[one, me_pz]
 
     def z_back(one):
-        for step in range(1, count_pz):
-            w_copy(one, step).wait_recv()
+        for c in range(PIECES):
+            for step in range(1, count_pz):
+                w_copy(PIECES * one + c, step).wait_recv()
         for g in range(0, groups, 2):
             rows = []
             for h in range(2):
-                rows += swap_blocks([w_in[one, q, g + h] for q in range(count_pz)], width)
+                rows += swap_blocks([
+                    w_in[PIECES * one + block % PIECES, block // PIECES, g + h]
+                    for block in range(blocks)
+                ], width)
             lines = from_right(jnp.concatenate(rows, axis=0), right_i[...])
-            lines = lines.reshape(2, count_pz, rows_y, n)
-            for h in range(2):
-                for block in range(count_pz):
+            lines = lines.reshape(2, blocks, rows_y, n)
+            for h in range(2):
+                for block in range(blocks):
                     x = block * groups + g + h
                     out[one, x] = conc[one, x] - lines[h, block]
 
+    z_forward(0)
+    y_forward(0)
+
     def opening(one, _):
         z_forward(one)
-
-        @pl.when(jnp.logical_and(one >= 1, one <= 2))
-        def _():
-            y_forward(one - 1)
-
         return 0
 
-    lax.fori_loop(0, species, opening, 0)
-    steps = species * slabs
+    lax.fori_loop(1, species, opening, 0)
+    y_forward(1)
+    steps = units * slabs
     lag = 2
 
     def middle(k, _):
@@ -403,11 +422,12 @@
         def _():
             x_both(k // slabs, lax.rem(k, slabs))
 
-        later = k // slabs + 2
-
-        @pl.when(jnp.logical_and(lax.rem(k, slabs) == 1, later < species))
-        def _():
-            y_forward(later)
+        for ahead in range(2):
+            later = 2 * k + 2 + ahead
+
+            @pl.when(later < units)
+            def _():
+                y_forward(later)
 
         back = k - lag
 
@@ -415,19 +435,22 @@
         def _():
             combine(back // slabs, lax.rem(back, slabs))
 
-        last = jnp.logical_and(back >= 0, lax.rem(k + slabs - lag, slabs) == slabs - 1)
-
-        @pl.when(jnp.logical_and(last, back < steps))
+        full = jnp.logical_and(back >= 0, lax.rem(back + 1, slabs) == 0)
+
+        @pl.when(jnp.logical_and(full, back < steps))
         def _():
             y_back(back // slabs)
 
-        @pl.when(jnp.logical_and(last, back >= slabs))
-        def _():
-            z_back(back // slabs - 1)
+        done = back - 2 * slabs + 1
+        whole = jnp.logical_and(done > 0, lax.rem(done, PIECES * slabs) == 0)
+
+        @pl.when(whole)
+        def _():
+            z_back(done // (PIECES * slabs) - 1)
 
         return 0
 
-    lax.fori_loop(0, steps + slabs + lag, middle, 0)
+    lax.fori_loop(0, steps + lag + 2 * slabs, middle, 0)
 
     for copy in pair:
         copy.wait_send()
@@ -452,7 +475,7 @@
 
         return 0
 
-    lax.fori_loop(0, species, drain, 0)
+    lax.fori_loop(0, units, drain, 0)
 
 
 def per_device_kernel(concentration, mobility, kappa, well_depth):
@@ -465,10 +488,11 @@
     orders = [blocks[[1, 0, 2, 3]].reshape(n), blocks[[2, 3, 1, 0]].reshape(n)]
     half_forward = np.stack([split_table(table[order[: n // 2]]).T for order in orders])
     half_inverse = np.stack([split_table(table[order].T).T for order in orders])
-    depths = jnp.broadcast_to(well_depth[:, None], (species, n))
-    groups = rows_x // count_pz
-    sub = n // count_py // count_pz
-    strip = rows_x * sub
+    blocks = count_pz * PIECES
+    units = species * PIECES
+    groups = rows_x // blocks
+    slabs = n // (blocks * SUBLANES)
+    strip = rows_x * SUBLANES
     f32 = jnp.float32
     vmem = pl.BlockSpec(memory_space=pltpu.VMEM)
     smem = pl.BlockSpec(memory_space=pltpu.SMEM)
@@ -476,35 +500,36 @@
     return pl.pallas_call(
         functools.partial(kernel, (count_py, count_pz)),
         out_shape=jax.ShapeDtypeStruct(concentration.shape, f32),
-        in_specs=[vmem, smem, smem] + [vmem] * 7,
+        in_specs=[vmem, smem, smem, smem] + [vmem] * 6,
         out_specs=vmem,
         scratch_shapes=[
             pltpu.VMEM((species, rows_x, rows_y, n), f32),
             pltpu.VMEM((species, n), f32),
-            pltpu.VMEM((2 * species, count_pz, groups, rows_y, n), f32),
-            pltpu.VMEM((2 * species, groups, n, n), f32),
-            pltpu.VMEM((2 * species, count_py, strip, n), f32),
-            pltpu.VMEM((2 * species, count_py, strip, n), f32),
-            pltpu.VMEM((species, count_py, 2 * strip, n), f32),
-            pltpu.VMEM((species, count_py, 2 * strip, n), f32),
-            pltpu.VMEM((species, count_py, 2 * strip, n), f32),
-            pltpu.VMEM((species, count_py, strip, n), f32),
-            pltpu.VMEM((species, count_py, strip, n), f32),
-            pltpu.VMEM((species, count_pz, groups, rows_y, n), f32),
-            pltpu.VMEM((species, count_pz, groups, rows_y, n), f32),
+            pltpu.VMEM((species, n), f32),
+            pltpu.VMEM((2 * units, count_pz, groups, rows_y, n), f32),
+            pltpu.VMEM((2 * units, groups, n, n), f32),
+            pltpu.VMEM((2 * units, slabs, strip, n), f32),
+            pltpu.VMEM((2 * units, slabs, strip, n), f32),
+            pltpu.VMEM((units, slabs, 2 * strip, n), f32),
+            pltpu.VMEM((units, slabs, 2 * strip, n), f32),
+            pltpu.VMEM((units, slabs, 2 * strip, n), f32),
+            pltpu.VMEM((units, slabs, strip, n), f32),
+            pltpu.VMEM((units, slabs, strip, n), f32),
+            pltpu.VMEM((units, count_pz, groups, rows_y, n), f32),
+            pltpu.VMEM((units, count_pz, groups, rows_y, n), f32),
             dma((2,)), dma((2,)),
-            dma((2 * species, count_pz)), dma((2 * species, count_pz)),
-            dma((2 * species, count_py)), dma((2 * species, count_py)),
-            dma((species, count_py)), dma((species, count_py)),
-            dma((species, count_py)), dma((species, count_py)),
-            dma((species, count_pz)), dma((species, count_pz)),
+            dma((2 * units, count_pz)), dma((2 * units, count_pz)),
+            dma((2 * units, slabs)), dma((2 * units, slabs)),
+            dma((units, slabs)), dma((units, slabs)),
+            dma((units, slabs)), dma((units, slabs)),
+            dma((units, count_pz)), dma((units, count_pz)),
         ],
         compiler_params=pltpu.CompilerParams(
             collective_id=0, has_side_effects=True, vmem_limit_bytes=60 * 1024 * 1024
         ),
         name="step",
     )(
-        concentration, mobility, kappa, depths,
+        concentration, mobility, kappa, well_depth,
         jnp.asarray(forward), jnp.asarray(inverse),
         jnp.asarray(forward.T), jnp.asarray(inverse.T),
         jnp.asarray(half_forward), jnp.asarray(half_inverse),
@@ -516,8 +541,9 @@
     count_sp, count_py, count_pz = (lax.axis_size(name) for name in ("sp", "py", "pz"))
     cube = rows_x * count_py == n and rows_y * count_pz == n and n == 128
     power = count_pz > 1 and count_pz & (count_pz - 1) == 0
-    whole = n % (8 * count_py * count_pz) == 0 and rows_x % (2 * count_pz) == 0 and rows_y % 8 == 0
-    if cube and power and whole and count_sp == 2 and count_py == 4 and concentration.shape[0] > 3:
+    blocks = count_pz * PIECES
+    whole = n % (SUBLANES * blocks) == 0 and rows_x % (2 * blocks) == 0 and rows_y % SUBLANES == 0
+    if cube and power and whole and count_sp == 2 and count_py == 4:
         return per_device_kernel(concentration, mobility, kappa, well_depth)
     return per_device_general(concentration, mobility, kappa, well_depth)
 

time: 153 us -> 140 us (0.915)
  Pallas kernels: 149 us -> 137 us
    pallas_call x1, Pallas kernels: 149 us -> 137 us  [per_device_kernel(): pl.pallas_call(functools.partial(kernel, (count_py, count_pz)), out_shape...]
where the time goes in v3:
time: 140 us
  Pallas kernels  137 us (98%)
  local copies, waits for them, and re-layouts  3.08 us (2%)
    pallas_call x1, Pallas kernels, per_device_kernel(): pl.pallas_call(functools.partial(kernel, (count_py, count_pz)), out_shape...  137 us
    unnamed x1, local copies, waits for them, and re-layouts  3.08 us

profile of v3, /device:TPU:0, one launch (start us, length us, event | category | flops | bytes accessed | tf_op | source)
XLA Modules:
  0.0 139.7 jit_solution(896279712163336944)
XLA Ops:
  0.0 136.6 %step.1 = f32[4,32,32,128]{3,2,1,0:T(8,128)} custom-call(f32[4,32,32,128]{3,2,1,0:T(8,128)} %conc.1, f32[8,8]{1,0:T(8,128)} %mobility.1, f32[8]{0:T(128)} %kappa.1, f32[4]{0:T(128)} %well_depth.1, bf16[256,256]{1,0:T(8,128)(2,1)} %constant.12.clone.right_f, bf16[256,256]{1,0:T(8,128)(2,1)} %constant.13.clone.right_i, ...), custom_call_target="tpu_custom_call" | custom-call | tf_op jit(solution)/shard_map/step/pallas_call | solution.py:500
  136.6 3.1 %copy.12 = f32[4,32,32,128]{3,2,1,0:T(8,128)} copy(f32[4,32,32,128]{3,2,1,0:T(8,128)} %step.1) | data formatting | bytes 4194304
